TPU v7x, 32 devices: a whole 2x2x4 slice. The times are simulated.
32 devices in a mesh: grp: 2 (over y), gx: 16 (over z, x, core), gy: 1.
Axes of the slice: x: 2, y: 2, z: 4, core: 2. Of those that a mesh axis runs over, the one named last changes fastest.
Arguments:
- residue_feats: bfloat16 [512, 256], P(('grp', 'gx')), parts along dimension 0, may hold values from -6 to 6
- pair_feats: bfloat16 [64, 512, 256], P(None, ('grp', 'gx'), 'gy'), parts along dimension 1, may hold values from -30 to 30
- w_row: bfloat16 [256, 64], replicated, may hold values from -0.375 to 0.375
- w_col: bfloat16 [256, 64], replicated, may hold values from -0.375 to 0.375
- first_taps: bfloat16 [9, 64, 64], replicated, may hold values from -0.25 to 0.25
- second_taps: bfloat16 [9, 64, 64], replicated, may hold values from -0.25 to 0.25
- norm_scale: float32 [2, 64], replicated, may hold values from 0.25 to 1.75
- norm_shift: float32 [2, 64], replicated, may hold values from -2 to 2
Outputs:
- symmetric: bfloat16 [64, 512, 256], P(None, ('grp', 'gx'), 'gy'), parts along dimension 1
There are 2 independent parts, one for each index of `grp`. A program takes and returns all parts, laid end to end along the dimension named above; an argument that names none is the same for every part. Nothing has to cross between parts.
All inputs are finite; a program needn't handle non-finite values.
Results may differ from a plain program's by a relative error of at most 0.012.
Values may be sent and summed in bfloat16 or wider, within the bound.
A program may use at most 64 MiB of HBM per device.

v0:
```python
import jax
import jax.numpy as jnp
from jax import lax
from jax.sharding import PartitionSpec as P

DILATION_STEP = 8
epsilon = 1e-05


def with_halo(cells, sides, width):
    for axis, dim in sides:
        count = lax.axis_size(axis)
        ends = count - 1
        head = lax.slice_in_dim(cells, 0, width, axis=dim)
        tail = lax.slice_in_dim(cells, cells.shape[dim] - width, cells.shape[dim], axis=dim)
        cells = jnp.concatenate(
            [
                lax.ppermute(tail, axis, [(i, (i + 1) % count) for i in range(ends)]),
                cells,
                lax.ppermute(head, axis, [((i + 1) % count, i) for i in range(ends)]),
            ],
            axis=dim,
        )
    return cells


def dilated(receptive_region, weights):
    row_count = receptive_region.shape[1]
    col_count = receptive_region.shape[2]
    border_padded_input = with_halo(receptive_region, (("gx", 1), ("gy", 2)), DILATION_STEP)
    tap_sum_total = jnp.zeros((weights.shape[1], row_count, col_count), jnp.float32)
    for filter_tap_index in range(9):
        row_displacement = filter_tap_index // 3 * DILATION_STEP
        column_displacement = filter_tap_index % 3 * DILATION_STEP
        window = border_padded_input[
            :,
            row_displacement : row_displacement + row_count,
            column_displacement : column_displacement + col_count,
        ]
        tap_sum_total = tap_sum_total + jnp.einsum(
            "oc,crw->orw", weights[filter_tap_index], window, preferred_element_type=jnp.float32
        )
    return tap_sum_total


def normalized(tap_sum_total, gain, shift):
    cell_count = (
        tap_sum_total.shape[1] * tap_sum_total.shape[2] * lax.axis_size("gx") * lax.axis_size("gy")
    )
    first_sum, second_sum = lax.psum(
        (jnp.sum(tap_sum_total, axis=(1, 2)), jnp.sum(tap_sum_total * tap_sum_total, axis=(1, 2))),
        ("gx", "gy"),
    )
    average = first_sum / cell_count
    spread = second_sum / cell_count - average * average
    centred = tap_sum_total - average[:, None, None]
    factor = gain * lax.rsqrt(spread + epsilon)
    return centred * factor[:, None, None] + shift[:, None, None]


def body(residue_feats, pair_feats, w_row, w_col, first_taps, second_taps, norm_scale, norm_shift):
    col_count = pair_feats.shape[2]
    col_start = lax.axis_index("gy") * col_count
    row_part = jnp.dot(residue_feats, w_row, preferred_element_type=jnp.float32).astype(
        jnp.bfloat16
    )
    everyone = lax.all_gather(residue_feats, "gx", axis=0, tiled=True)
    col_feats = lax.dynamic_slice_in_dim(everyone, col_start, col_count, 0)
    col_part = jnp.dot(col_feats, w_col, preferred_element_type=jnp.float32).astype(jnp.bfloat16)
    block_in = (
        pair_feats.astype(jnp.float32)
        + row_part.T.astype(jnp.float32)[:, :, None]
        + col_part.T.astype(jnp.float32)[:, None, :]
    ).astype(jnp.bfloat16)
    first_conv = dilated(block_in, first_taps)
    activated = jax.nn.elu(normalized(first_conv, norm_scale[0], norm_shift[0])).astype(
        jnp.bfloat16
    )
    second_conv = dilated(activated, second_taps)
    block_out = jax.nn.elu(
        block_in.astype(jnp.float32) + normalized(second_conv, norm_scale[1], norm_shift[1])
    ).astype(jnp.bfloat16)
    whole_rows = lax.all_gather(block_out, "gy", axis=2, tiled=True)
    columns = lax.all_to_all(whole_rows, "gx", split_axis=2, concat_axis=1, tiled=True)
    flipped = lax.dynamic_slice_in_dim(columns, col_start, col_count, 1)
    mirrored = jnp.transpose(flipped, (0, 2, 1))
    return (0.5 * (block_out.astype(jnp.float32) + mirrored.astype(jnp.float32))).astype(
        jnp.bfloat16
    )


def solution(mesh):
    placed = (P(("grp", "gx"), None), P(None, ("grp", "gx"), "gy"), P(), P(), P(), P(), P(), P())
    return jax.shard_map(
        body, mesh=mesh, in_specs=placed, out_specs=P(None, ("grp", "gx"), "gy"), check_vma=False
    )
```

profile of v0, /device:TPU:0, one launch (start us, length us, event | category | flops | bytes accessed | tf_op | source)
XLA Modules:
  0.0 140.1 jit_solution(18333366935052121485)
XLA Ops:
  0.0 23.8 %all_gather.4 = bf16[256,256]{1,0:T(8,128)(2,1)S(1)} all-gather(bf16[16,256]{1,0:T(8,128)(2,1)} %param.8), channel_id=1, replica_groups=mesh['grp'=2,'gx'=16,'gy'=1] {'gx'}, dimensions={0}, use_global_device_ids=true | all-gather | bytes 139264 | tf_op jit(solution)/shard_map/all_gather | solution.py:67
  23.8 0.9 fusion.13
  24.9 1.3 add_convert_fusion
  26.2 2.3 %collective-permute-start = (bf16[64,8,256]{2,0,1:T(8,128)(2,1)S(1)}, bf16[64,8,256]{2,0,1:T(8,128)(2,1)S(1)}, u32[]{:S(2)}, u32[]{:S(2)}) collective-permute-start(bf16[64,8,256]{2,0,1:T(8,128)(2,1)S(1)} %get-tuple-element.23), channel_id=1, source_target_pairs={{0,1},{1,2},{2,3},{3,4},{4,5},{5,6},{6,7},{7,8},{8,9},{9,10},{10,1... | collective-permute-start | bytes 786440 | tf_op jit(solution)/shard_map/ppermute | solution.py:18
  28.5 1.3 collective-permute-start.1
  29.8 0.3 fusion.62
  30.1 1.8 %collective-permute-done.1 = bf16[64,8,256]{2,0,1:T(8,128)(2,1)S(1)} collective-permute-done((bf16[64,8,256]{2,0,1:T(8,128)(2,1)S(1)}, bf16[64,8,256]{2,0,1:T(8,128)(2,1)S(1)}, u32[]{:S(2)}, u32[]{:S(2)}) %collective-permute-start.1) | collective-permute-done | bytes 262176 | tf_op jit(solution)/shard_map/ppermute | solution.py:20
  32.1 0.3 fusion.93
  32.3 0.7 collective-permute-start.2
  33.0 0.7 collective-permute-start.3
  33.7 0.3 fusion.45
  34.0 0.3 fusion.36
  34.3 1.3 maximum_maximum_fusion
  35.6 0.4 fusion.43
  36.0 0.4 fusion.34
  36.4 0.3 fusion.41
  36.7 0.3 fusion.38
  36.9 0.4 fusion.11
  37.3 0.7 fusion.91
  38.0 33.9 %all-reduce.1 = (f32[64]{0:T(128)S(1)}, f32[64]{0:T(128)S(1)}) all-reduce(f32[64]{0:T(128)S(1)} %get-tuple-element.8, f32[64]{0:T(128)S(1)} %get-tuple-element.7), channel_id=1, replica_groups=mesh['grp'=2,'gx'=16,'gy'=1] {'gx','gy'}, use_global_device_ids=true, to_apply=%region_3.0 | all-reduce | flops 128 | bytes 1024 | tf_op jit(solution)/shard_map/psum | solution.py:50
  72.0 0.6 fusion.15
  72.6 1.3 collective-permute-start.4
  73.9 1.3 collective-permute-start.5
  75.2 0.3 fusion.52
  75.5 1.8 %collective-permute-done.5 = bf16[64,8,256]{2,0,1:T(8,128)(2,1)S(1)} collective-permute-done((bf16[64,8,256]{2,0,1:T(8,128)(2,1)S(1)}, bf16[64,8,256]{2,0,1:T(8,128)(2,1)S(1)}, u32[]{:S(2)}, u32[]{:S(2)}) %collective-permute-start.5) | collective-permute-done | bytes 262176 | tf_op jit(solution)/shard_map/ppermute | solution.py:20
  77.5 0.3 fusion.92
  77.8 0.7 collective-permute-start.6
  78.5 0.7 collective-permute-start.7
  79.2 0.3 fusion.31
  79.4 0.3 fusion.22
  79.7 1.3 maximum_maximum_fusion.1
  81.0 0.4 fusion.29
  81.4 0.4 fusion.20
  81.8 0.3 fusion.27
  82.1 0.3 fusion.24
  82.3 0.4 fusion.5
  82.8 0.7 fusion.90
  83.4 31.5 %all-reduce = (f32[64]{0:T(128)S(1)}, f32[64]{0:T(128)S(1)}) all-reduce(f32[64]{0:T(128)S(1)} %get-tuple-element.6, f32[64]{0:T(128)S(1)} %get-tuple-element.5), channel_id=1, replica_groups=mesh['grp'=2,'gx'=16,'gy'=1] {'gx','gy'}, use_global_device_ids=true, to_apply=%region_7.8 | all-reduce | flops 128 | bytes 1024 | tf_op jit(solution)/shard_map/psum | solution.py:50
  115.0 0.7 fusion.17
  115.7 1.0 copy.18
  116.7 0.7 reshape.32
  117.4 16.9 %all_to_all.4 = bf16[16,2,8192]{2,1,0:T(2,128)(2,1)S(1)} all-to-all(bf16[16,2,8192]{2,1,0:T(2,128)(2,1)S(1)} %reshape.32), channel_id=1, replica_groups=mesh['grp'=2,'gx'=16,'gy'=1] {'gx'}, dimensions={0} | all-to-all | bytes 1048576 | tf_op jit(solution)/shard_map/all_to_all | solution.py:84
  134.3 0.7 reshape.33
  135.0 0.3 copy.19
  135.2 0.2 convert_bitcast_fusion
  135.7 2.0 %copy.21 = f32[64,256,16]{1,0,2:T(8,128)} copy(f32[64,256,16]{0,2,1:T(8,128)S(1)} %bitcast.109) | data formatting | bytes 2097152 | tf_op jit(solution)/shard_map/convert_element_type | solution.py:87
  137.6 1.4 fusion.19
  139.0 1.1 copy.22
  (27 shorter events, 0.8 us)
Async XLA Ops:
  0.0 24.7 %copy-start = (bf16[256,64]{0,1:T(8,128)(2,1)S(1)}, bf16[256,64]{0,1:T(8,128)(2,1)}, u32[]{:S(2)}) copy-start(bf16[256,64]{0,1:T(8,128)(2,1)} %param.11) | copy-start | bytes 98308
  0.0 29.8 %copy-start.5 = (f32[2,64]{1,0:T(2,128)S(1)}, f32[2,64]{1,0:T(2,128)}, u32[]{:S(2)}) copy-start(f32[2,64]{1,0:T(2,128)} %param.15) | copy-start | bytes 1540
  0.0 29.8 %copy-start.2 = (bf16[9,64,64]{2,1,0:T(8,128)(2,1)S(1)}, bf16[9,64,64]{2,1,0:T(8,128)(2,1)}, u32[]{:S(2)}) copy-start(bf16[9,64,64]{2,1,0:T(8,128)(2,1)} %param.12) | copy-start | bytes 221188
  26.2 3.9 %collective-permute-start = (bf16[64,8,256]{2,0,1:T(8,128)(2,1)S(1)}, bf16[64,8,256]{2,0,1:T(8,128)(2,1)S(1)}, u32[]{:S(2)}, u32[]{:S(2)}) collective-permute-start(bf16[64,8,256]{2,0,1:T(8,128)(2,1)S(1)} %get-tuple-element.23), channel_id=1, source_target_pairs={{0,1},{1,2},{2,3},{3,4},{4,5},{5,6},{6,7},{7,8},{8,9},{9,10},{10,1... | collective-permute-start | bytes 786440 | tf_op jit(solution)/shard_map/ppermute | solution.py:18
  28.5 3.4 %collective-permute-start.1 = (bf16[64,8,256]{2,0,1:T(8,128)(2,1)S(1)}, bf16[64,8,256]{2,0,1:T(8,128)(2,1)S(1)}, u32[]{:S(2)}, u32[]{:S(2)}) collective-permute-start(bf16[64,8,256]{2,0,1:T(8,128)(2,1)S(1)} %get-tuple-element.24), channel_id=1, source_target_pairs={{1,0},{2,1},{3,2},{4,3},{5,4},{6,5},{7,6},{8,7},{9,8},{10,9},{11,1... | collective-permute-start | bytes 786440 | tf_op jit(solution)/shard_map/ppermute | solution.py:20
  32.3 1.9 %collective-permute-start.2 = (bf16[64,32,8]{2,0,1:T(8,128)(2,1)S(1)}, bf16[64,32,8]{2,0,1:T(8,128)(2,1)S(1)}, u32[]{:S(2)}, u32[]{:S(2)}) collective-permute-start(bf16[64,32,8]{2,0,1:T(8,128)(2,1)S(1)} %get-tuple-element.19), channel_id=1, source_target_pairs={} | collective-permute-start | bytes 98312 | tf_op jit(solution)/shard_map/ppermute | solution.py:18
  33.0 1.3 collective-permute-start.3
  37.3 34.6 %copy-start.4 = (f32[2,64]{1,0:T(2,128)S(1)}, f32[2,64]{1,0:T(2,128)}, u32[]{:S(2)}) copy-start(f32[2,64]{1,0:T(2,128)} %param.14) | copy-start | bytes 1540
  38.0 37.2 %copy-start.3 = (bf16[9,64,64]{2,1,0:T(8,128)(2,1)S(1)}, bf16[9,64,64]{2,1,0:T(8,128)(2,1)}, u32[]{:S(2)}) copy-start(bf16[9,64,64]{2,1,0:T(8,128)(2,1)} %param.13) | copy-start | bytes 221188
  72.6 2.9 %collective-permute-start.4 = (bf16[64,8,256]{2,0,1:T(8,128)(2,1)S(1)}, bf16[64,8,256]{2,0,1:T(8,128)(2,1)S(1)}, u32[]{:S(2)}, u32[]{:S(2)}) collective-permute-start(bf16[64,8,256]{2,0,1:T(8,128)(2,1)S(1)} %get-tuple-element.21), channel_id=1, source_target_pairs={{0,1},{1,2},{2,3},{3,4},{4,5},{5,6},{6,7},{7,8},{8,9},{9,10},{10,1... | collective-permute-start | bytes 786440 | tf_op jit(solution)/shard_map/ppermute | solution.py:18
  73.9 3.4 %collective-permute-start.5 = (bf16[64,8,256]{2,0,1:T(8,128)(2,1)S(1)}, bf16[64,8,256]{2,0,1:T(8,128)(2,1)S(1)}, u32[]{:S(2)}, u32[]{:S(2)}) collective-permute-start(bf16[64,8,256]{2,0,1:T(8,128)(2,1)S(1)} %get-tuple-element.22), channel_id=1, source_target_pairs={{1,0},{2,1},{3,2},{4,3},{5,4},{6,5},{7,6},{8,7},{9,8},{10,9},{11,1... | collective-permute-start | bytes 786440 | tf_op jit(solution)/shard_map/ppermute | solution.py:20
  77.8 1.9 %collective-permute-start.6 = (bf16[64,32,8]{2,0,1:T(8,128)(2,1)S(1)}, bf16[64,32,8]{2,0,1:T(8,128)(2,1)S(1)}, u32[]{:S(2)}, u32[]{:S(2)}) collective-permute-start(bf16[64,32,8]{2,0,1:T(8,128)(2,1)S(1)} %get-tuple-element.15), channel_id=1, source_target_pairs={} | collective-permute-start | bytes 98312 | tf_op jit(solution)/shard_map/ppermute | solution.py:18
  78.5 1.3 collective-permute-start.7
  82.7 32.2 %copy-start.1 = (bf16[64,16,256]{2,1,0:T(8,128)(2,1)S(1)}, bf16[64,16,256]{2,1,0:T(8,128)(2,1)}, u32[]{:S(2)}) copy-start(bf16[64,16,256]{2,1,0:T(8,128)(2,1)} %param.9) | copy-start | bytes 1572868
where the time goes:
time: 141 us; the launch traced here: 140 us
  blocking collectives  106 us (75%)
  starting transfers between devices  8.9 us (6%)
  matrix products  7.38 us (5%)
  other arithmetic  7.08 us (5%)
  local copies, waits for them, and re-layouts  6.52 us (5%)
  waiting for transfers between devices  3.66 us (3%)
    psum x2, blocking collectives, normalized(): lax.psum((jnp.sum(tap_sum_total, axis=(1, 2)), jnp.sum(tap_sum_total * ta...  65.5 us
    all_gather x1, blocking collectives, body(): everyone = lax.all_gather(residue_feats, 'gx', axis=0, tiled=True)  23.8 us
    all_to_all x1, blocking collectives, body(): lax.all_to_all(whole_rows, 'gx', split_axis=2, concat_axis=1, tiled=True)  16.9 us
    dot_general x18, matrix products, dilated(): jnp.einsum('oc,crw->orw', weights[filter_tap_index], window, preferred_el...  6.34 us
    ppermute x4, starting transfers between devices, with_halo(): lax.ppermute(tail, axis, [(i, (i + 1) % count) for i in range(ends)])  4.94 us
    ppermute x4, starting transfers between devices, with_halo(): lax.ppermute(head, axis, [((i + 1) % count, i) for i in range(ends)])  3.96 us
    ppermute x4, waiting for transfers between devices, with_halo(): lax.ppermute(head, axis, [((i + 1) % count, i) for i in range(ends)])  3.65 us
    concatenate x4, other arithmetic, with_halo(): jnp.concatenate([lax.ppermute(tail, axis, [(i, (i + 1) % count) for i in...  2.87 us
  transfers between devices with their start and end apart: 8, of which 2 were waited for; matrix products, arithmetic and copies ran while one was open for 1% of the time, Pallas kernels for 0%

commit v1 on v0

--- a/solution.py
+++ b/solution.py
@@ -5,6 +5,22 @@
 
 DILATION_STEP = 8
 epsilon = 1e-05
+
+
+def collect(x, axis, dim):
+    ways, here, step = (lax.axis_size(axis), lax.axis_index(axis), x.shape[dim])
+    lengths = [n * ways if d == dim else n for d, n in enumerate(x.shape)]
+    full = lax.dynamic_update_slice_in_dim(jnp.zeros(lengths, x.dtype), x, here * step, axis=dim)
+    going_up = going_down = x
+    for far in range(1, ways // 2 + 1):
+        going_up = lax.ppermute(going_up, axis, [(d, (d + 1) % ways) for d in range(ways)])
+        full = lax.dynamic_update_slice_in_dim(full, going_up, (here - far) % ways * step, axis=dim)
+        if 2 * far < ways:
+            going_down = lax.ppermute(going_down, axis, [(d, (d - 1) % ways) for d in range(ways)])
+            full = lax.dynamic_update_slice_in_dim(
+                full, going_down, (here + far) % ways * step, axis=dim
+            )
+    return full
 
 
 def with_halo(cells, sides, width):
@@ -64,7 +80,7 @@
     row_part = jnp.dot(residue_feats, w_row, preferred_element_type=jnp.float32).astype(
         jnp.bfloat16
     )
-    everyone = lax.all_gather(residue_feats, "gx", axis=0, tiled=True)
+    everyone = collect(residue_feats, "gx", 0)
     col_feats = lax.dynamic_slice_in_dim(everyone, col_start, col_count, 0)
     col_part = jnp.dot(col_feats, w_col, preferred_element_type=jnp.float32).astype(jnp.bfloat16)
     block_in = (

time: 141 us -> 162 us (1.15)
  starting transfers between devices: 8.9 us -> 40.1 us
  blocking collectives: 106 us -> 80.7 us
  waiting for transfers between devices: 3.66 us -> 17.6 us
    ppermute x0 -> x15, starting transfers between devices: none -> 32 us  [the longest x7 31.5 us: collect(): lax.ppermute(going_down, axis, [(d, (d - 1) % ways) for d in range(ways)])]
    all_gather x1 -> x0, blocking collectives: 23.8 us -> none  [body(): everyone = lax.all_gather(residue_feats, 'gx', axis=0, tiled=True)]
    ppermute x0 -> x15, waiting for transfers between devices: none -> 13.9 us  [the longest x8 13.7 us: collect(): lax.ppermute(going_up, axis, [(d, (d + 1) % ways) for d in range(ways)])]
  transfers between devices with their start and end apart: 8 -> 23, of which waited for: 2 -> 9; matrix products, arithmetic and copies ran while one was open for 1% -> 3% of each run, Pallas kernels for 0% -> 0%
where the time goes in v1:
time: 162 us; the launch traced here: 161 us
  blocking collectives  80.7 us (50%)
  starting transfers between devices  40.1 us (25%)
  waiting for transfers between devices  17.6 us (11%)
  local copies, waits for them, and re-layouts  8.05 us (5%)
  matrix products  7.4 us (5%)
  other arithmetic  7.08 us (4%)
    psum x2, blocking collectives, normalized(): lax.psum((jnp.sum(tap_sum_total, axis=(1, 2)), jnp.sum(tap_sum_total * ta...  63.8 us
    ppermute x7, starting transfers between devices, collect(): lax.ppermute(going_down, axis, [(d, (d - 1) % ways) for d in range(ways)])  31.5 us
    all_to_all x1, blocking collectives, body(): lax.all_to_all(whole_rows, 'gx', split_axis=2, concat_axis=1, tiled=True)  16.9 us
    ppermute x8, waiting for transfers between devices, collect(): lax.ppermute(going_up, axis, [(d, (d + 1) % ways) for d in range(ways)])  13.7 us
    dot_general x18, matrix products, dilated(): jnp.einsum('oc,crw->orw', weights[filter_tap_index], window, preferred_el...  6.33 us
    ppermute x4, starting transfers between devices, with_halo(): lax.ppermute(tail, axis, [(i, (i + 1) % count) for i in range(ends)])  4.18 us
    ppermute x4, starting transfers between devices, with_halo(): lax.ppermute(head, axis, [((i + 1) % count, i) for i in range(ends)])  3.96 us
    ppermute x4, waiting for transfers between devices, with_halo(): lax.ppermute(head, axis, [((i + 1) % count, i) for i in range(ends)])  3.67 us
  transfers between devices with their start and end apart: 23, of which 9 were waited for; matrix products, arithmetic and copies ran while one was open for 3% of the time, Pallas kernels for 0%

profile of v1, /device:TPU:0, one launch (start us, length us, event | category | flops | bytes accessed | tf_op | source)
XLA Modules:
  0.0 161.4 jit_solution(11027126331277012322)
XLA Ops:
  0.0 0.5 collective-permute-start
  0.5 5.0 %collective-permute-start.1 = (bf16[16,256]{1,0:T(8,128)(2,1)}, bf16[16,256]{1,0:T(8,128)(2,1)S(1)}, u32[]{:S(2)}, u32[]{:S(2)}) collective-permute-start(bf16[16,256]{1,0:T(8,128)(2,1)} %param.8), channel_id=1, source_target_pairs={{0,15},{1,0},{2,1},{3,2},{4,3},{5,4},{6,5},{7,6},{8,7},{9,8},{10,9... | collective-permute-start | bytes 24584 | tf_op jit(solution)/shard_map/ppermute | solution.py:19
  5.5 0.9 fusion.14
  6.4 0.8 slice_bitcast_fusion
  7.2 0.7 constant_dynamic-update-slice_fusion.15
  7.9 4.4 %collective-permute-start.3 = (bf16[16,256]{1,0:T(8,128)(2,1)S(1)}, bf16[16,256]{1,0:T(8,128)(2,1)S(1)}, u32[]{:S(2)}, u32[]{:S(2)}) collective-permute-start(bf16[16,256]{1,0:T(8,128)(2,1)S(1)} %collective-permute-done.1), channel_id=1, source_target_pairs={{0,15},{1,0},{2,1},{3,2},{4,3},{5,4},{6,5},{7,6},{8,7},{9,8},{10,9... | collective-permute-start | bytes 24584 | tf_op jit(solution)/shard_map/ppermute | solution.py:19
  12.4 1.3 collective-permute-done.2
  13.7 4.4 %collective-permute-start.5 = (bf16[16,256]{1,0:T(8,128)(2,1)S(1)}, bf16[16,256]{1,0:T(8,128)(2,1)S(1)}, u32[]{:S(2)}, u32[]{:S(2)}) collective-permute-start(bf16[16,256]{1,0:T(8,128)(2,1)S(1)} %collective-permute-done.3), channel_id=1, source_target_pairs={{0,15},{1,0},{2,1},{3,2},{4,3},{5,4},{6,5},{7,6},{8,7},{9,8},{10,9... | collective-permute-start | bytes 24584 | tf_op jit(solution)/shard_map/ppermute | solution.py:19
  18.1 1.3 collective-permute-done.4
  19.5 4.4 %collective-permute-start.7 = (bf16[16,256]{1,0:T(8,128)(2,1)S(1)}, bf16[16,256]{1,0:T(8,128)(2,1)S(1)}, u32[]{:S(2)}, u32[]{:S(2)}) collective-permute-start(bf16[16,256]{1,0:T(8,128)(2,1)S(1)} %collective-permute-done.5), channel_id=1, source_target_pairs={{0,15},{1,0},{2,1},{3,2},{4,3},{5,4},{6,5},{7,6},{8,7},{9,8},{10,9... | collective-permute-start | bytes 24584 | tf_op jit(solution)/shard_map/ppermute | solution.py:19
  23.9 1.3 collective-permute-done.6
  25.3 4.4 %collective-permute-start.9 = (bf16[16,256]{1,0:T(8,128)(2,1)S(1)}, bf16[16,256]{1,0:T(8,128)(2,1)S(1)}, u32[]{:S(2)}, u32[]{:S(2)}) collective-permute-start(bf16[16,256]{1,0:T(8,128)(2,1)S(1)} %collective-permute-done.7), channel_id=1, source_target_pairs={{0,15},{1,0},{2,1},{3,2},{4,3},{5,4},{6,5},{7,6},{8,7},{9,8},{10,9... | collective-permute-start | bytes 24584 | tf_op jit(solution)/shard_map/ppermute | solution.py:19
  29.7 1.3 collective-permute-done.8
  31.1 4.4 %collective-permute-start.11 = (bf16[16,256]{1,0:T(8,128)(2,1)S(1)}, bf16[16,256]{1,0:T(8,128)(2,1)S(1)}, u32[]{:S(2)}, u32[]{:S(2)}) collective-permute-start(bf16[16,256]{1,0:T(8,128)(2,1)S(1)} %collective-permute-done.9), channel_id=1, source_target_pairs={{0,15},{1,0},{2,1},{3,2},{4,3},{5,4},{6,5},{7,6},{8,7},{9,8},{10,9... | collective-permute-start | bytes 24584 | tf_op jit(solution)/shard_map/ppermute | solution.py:19
  35.5 1.3 collective-permute-done.10
  36.8 4.4 %collective-permute-start.13 = (bf16[16,256]{1,0:T(8,128)(2,1)S(1)}, bf16[16,256]{1,0:T(8,128)(2,1)S(1)}, u32[]{:S(2)}, u32[]{:S(2)}) collective-permute-start(bf16[16,256]{1,0:T(8,128)(2,1)S(1)} %collective-permute-done.11), channel_id=1, source_target_pairs={{0,15},{1,0},{2,1},{3,2},{4,3},{5,4},{6,5},{7,6},{8,7},{9,8},{10,9... | collective-permute-start | bytes 24584 | tf_op jit(solution)/shard_map/ppermute | solution.py:19
  41.2 1.3 collective-permute-done.12
  42.6 5.7 %collective-permute-done.14 = bf16[16,256]{1,0:T(8,128)(2,1)S(1)} collective-permute-done((bf16[16,256]{1,0:T(8,128)(2,1)S(1)}, bf16[16,256]{1,0:T(8,128)(2,1)S(1)}, u32[]{:S(2)}, u32[]{:S(2)}) %collective-permute-start.14) | collective-permute-done | bytes 8224 | tf_op jit(solution)/shard_map/ppermute | solution.py:16
  48.5 1.3 add_convert_fusion
  49.8 1.3 collective-permute-start.15
  51.2 1.3 collective-permute-start.16
  52.8 1.8 %collective-permute-done.16 = bf16[64,8,256]{2,0,1:T(8,128)(2,1)S(1)} collective-permute-done((bf16[64,8,256]{2,0,1:T(8,128)(2,1)S(1)}, bf16[64,8,256]{2,0,1:T(8,128)(2,1)S(1)}, u32[]{:S(2)}, u32[]{:S(2)}) %collective-permute-start.16) | collective-permute-done | bytes 262176 | tf_op jit(solution)/shard_map/ppermute | solution.py:36
  55.0 0.7 collective-permute-start.17
  55.7 0.7 collective-permute-start.18
  57.0 1.3 maximum_maximum_fusion
  58.7 0.4 fusion.35
  59.6 0.4 fusion.11
  60.0 0.7 fusion.92
  60.7 29.9 %all-reduce.1 = (f32[64]{0:T(128)S(1)}, f32[64]{0:T(128)S(1)}) all-reduce(f32[64]{0:T(128)S(1)} %get-tuple-element.8, f32[64]{0:T(128)S(1)} %get-tuple-element.7), channel_id=1, replica_groups=mesh['grp'=2,'gx'=16,'gy'=1] {'gx','gy'}, use_global_device_ids=true, to_apply=%region_3.4 | all-reduce | flops 128 | bytes 1024 | tf_op jit(solution)/shard_map/psum | solution.py:66
  90.6 0.6 fusion.16
  91.2 1.5 collective-permute-start.19
  92.8 1.3 collective-permute-start.20
  94.3 1.8 %collective-permute-done.20 = bf16[64,8,256]{2,0,1:T(8,128)(2,1)S(1)} collective-permute-done((bf16[64,8,256]{2,0,1:T(8,128)(2,1)S(1)}, bf16[64,8,256]{2,0,1:T(8,128)(2,1)S(1)}, u32[]{:S(2)}, u32[]{:S(2)}) %collective-permute-start.20) | collective-permute-done | bytes 262176 | tf_op jit(solution)/shard_map/ppermute | solution.py:36
  96.6 0.7 collective-permute-start.21
  97.3 0.7 collective-permute-start.22
  98.6 1.3 maximum_maximum_fusion.1
  100.2 0.4 fusion.21
  101.2 0.4 fusion.5
  101.6 0.7 fusion.91
  102.3 33.9 %all-reduce = (f32[64]{0:T(128)S(1)}, f32[64]{0:T(128)S(1)}) all-reduce(f32[64]{0:T(128)S(1)} %get-tuple-element.6, f32[64]{0:T(128)S(1)} %get-tuple-element.5), channel_id=1, replica_groups=mesh['grp'=2,'gx'=16,'gy'=1] {'gx','gy'}, use_global_device_ids=true, to_apply=%region_7.8 | all-reduce | flops 128 | bytes 1024 | tf_op jit(solution)/shard_map/psum | solution.py:66
  136.2 0.7 fusion.18
  136.9 1.0 copy.18
  137.9 0.7 reshape.32
  138.6 16.9 %all_to_all.4 = bf16[16,2,8192]{2,1,0:T(2,128)(2,1)S(1)} all-to-all(bf16[16,2,8192]{2,1,0:T(2,128)(2,1)S(1)} %reshape.32), channel_id=1, replica_groups=mesh['grp'=2,'gx'=16,'gy'=1] {'gx'}, dimensions={0} | all-to-all | bytes 1048576 | tf_op jit(solution)/shard_map/all_to_all | solution.py:100
  155.5 0.7 reshape.33
  156.9 2.0 %copy.21 = f32[64,256,16]{1,0,2:T(8,128)} copy(f32[64,256,16]{0,2,1:T(8,128)S(1)} %bitcast.111) | data formatting | bytes 2097152 | tf_op jit(solution)/shard_map/convert_element_type | solution.py:103
  158.9 1.4 fusion.20
  160.3 1.1 copy.22
  (71 shorter events, 5.5 us)
Async XLA Ops:
  0.0 48.3 %copy-start = (bf16[256,64]{0,1:T(8,128)(2,1)S(1)}, bf16[256,64]{0,1:T(8,128)(2,1)}, u32[]{:S(2)}) copy-start(bf16[256,64]{0,1:T(8,128)(2,1)} %param.11) | copy-start | bytes 98308
  0.0 7.9 %collective-permute-start = (bf16[16,256]{1,0:T(8,128)(2,1)}, bf16[16,256]{1,0:T(8,128)(2,1)S(1)}, u32[]{:S(2)}, u32[]{:S(2)}) collective-permute-start(bf16[16,256]{1,0:T(8,128)(2,1)} %param.8), channel_id=1, source_target_pairs={{0,1},{1,2},{2,3},{3,4},{4,5},{5,6},{6,7},{7,8},{8,9},{9,10},{10,1... | collective-permute-start | bytes 24584 | tf_op jit(solution)/shard_map/ppermute | solution.py:16
  0.5 7.4 %collective-permute-start.1 = (bf16[16,256]{1,0:T(8,128)(2,1)}, bf16[16,256]{1,0:T(8,128)(2,1)S(1)}, u32[]{:S(2)}, u32[]{:S(2)}) collective-permute-start(bf16[16,256]{1,0:T(8,128)(2,1)} %param.8), channel_id=1, source_target_pairs={{0,15},{1,0},{2,1},{3,2},{4,3},{5,4},{6,5},{7,6},{8,7},{9,8},{10,9... | collective-permute-start | bytes 24584 | tf_op jit(solution)/shard_map/ppermute | solution.py:19
  5.5 47.0 %copy-start.2 = (bf16[9,64,64]{2,1,0:T(8,128)(2,1)S(1)}, bf16[9,64,64]{2,1,0:T(8,128)(2,1)}, u32[]{:S(2)}) copy-start(bf16[9,64,64]{2,1,0:T(8,128)(2,1)} %param.12) | copy-start | bytes 221188
  7.9 5.8 %collective-permute-start.2 = (bf16[16,256]{1,0:T(8,128)(2,1)S(1)}, bf16[16,256]{1,0:T(8,128)(2,1)S(1)}, u32[]{:S(2)}, u32[]{:S(2)}) collective-permute-start(bf16[16,256]{1,0:T(8,128)(2,1)S(1)} %collective-permute-done), channel_id=1, source_target_pairs={{0,1},{1,2},{2,3},{3,4},{4,5},{5,6},{6,7},{7,8},{8,9},{9,10},{10,1... | collective-permute-start | bytes 24584 | tf_op jit(solution)/shard_map/ppermute | solution.py:16
  7.9 5.8 %collective-permute-start.3 = (bf16[16,256]{1,0:T(8,128)(2,1)S(1)}, bf16[16,256]{1,0:T(8,128)(2,1)S(1)}, u32[]{:S(2)}, u32[]{:S(2)}) collective-permute-start(bf16[16,256]{1,0:T(8,128)(2,1)S(1)} %collective-permute-done.1), channel_id=1, source_target_pairs={{0,15},{1,0},{2,1},{3,2},{4,3},{5,4},{6,5},{7,6},{8,7},{9,8},{10,9... | collective-permute-start | bytes 24584 | tf_op jit(solution)/shard_map/ppermute | solution.py:19
  13.7 5.8 %collective-permute-start.4 = (bf16[16,256]{1,0:T(8,128)(2,1)S(1)}, bf16[16,256]{1,0:T(8,128)(2,1)S(1)}, u32[]{:S(2)}, u32[]{:S(2)}) collective-permute-start(bf16[16,256]{1,0:T(8,128)(2,1)S(1)} %collective-permute-done.2), channel_id=1, source_target_pairs={{0,1},{1,2},{2,3},{3,4},{4,5},{5,6},{6,7},{7,8},{8,9},{9,10},{10,1... | collective-permute-start | bytes 24584 | tf_op jit(solution)/shard_map/ppermute | solution.py:16
  13.7 5.8 %collective-permute-start.5 = (bf16[16,256]{1,0:T(8,128)(2,1)S(1)}, bf16[16,256]{1,0:T(8,128)(2,1)S(1)}, u32[]{:S(2)}, u32[]{:S(2)}) collective-permute-start(bf16[16,256]{1,0:T(8,128)(2,1)S(1)} %collective-permute-done.3), channel_id=1, source_target_pairs={{0,15},{1,0},{2,1},{3,2},{4,3},{5,4},{6,5},{7,6},{8,7},{9,8},{10,9... | collective-permute-start | bytes 24584 | tf_op jit(solution)/shard_map/ppermute | solution.py:19
  19.5 5.8 %collective-permute-start.6 = (bf16[16,256]{1,0:T(8,128)(2,1)S(1)}, bf16[16,256]{1,0:T(8,128)(2,1)S(1)}, u32[]{:S(2)}, u32[]{:S(2)}) collective-permute-start(bf16[16,256]{1,0:T(8,128)(2,1)S(1)} %collective-permute-done.4), channel_id=1, source_target_pairs={{0,1},{1,2},{2,3},{3,4},{4,5},{5,6},{6,7},{7,8},{8,9},{9,10},{10,1... | collective-permute-start | bytes 24584 | tf_op jit(solution)/shard_map/ppermute | solution.py:16
  19.5 5.8 %collective-permute-start.7 = (bf16[16,256]{1,0:T(8,128)(2,1)S(1)}, bf16[16,256]{1,0:T(8,128)(2,1)S(1)}, u32[]{:S(2)}, u32[]{:S(2)}) collective-permute-start(bf16[16,256]{1,0:T(8,128)(2,1)S(1)} %collective-permute-done.5), channel_id=1, source_target_pairs={{0,15},{1,0},{2,1},{3,2},{4,3},{5,4},{6,5},{7,6},{8,7},{9,8},{10,9... | collective-permute-start | bytes 24584 | tf_op jit(solution)/shard_map/ppermute | solution.py:19
  25.2 5.8 %collective-permute-start.8 = (bf16[16,256]{1,0:T(8,128)(2,1)S(1)}, bf16[16,256]{1,0:T(8,128)(2,1)S(1)}, u32[]{:S(2)}, u32[]{:S(2)}) collective-permute-start(bf16[16,256]{1,0:T(8,128)(2,1)S(1)} %collective-permute-done.6), channel_id=1, source_target_pairs={{0,1},{1,2},{2,3},{3,4},{4,5},{5,6},{6,7},{7,8},{8,9},{9,10},{10,1... | collective-permute-start | bytes 24584 | tf_op jit(solution)/shard_map/ppermute | solution.py:16
  25.3 5.8 %collective-permute-start.9 = (bf16[16,256]{1,0:T(8,128)(2,1)S(1)}, bf16[16,256]{1,0:T(8,128)(2,1)S(1)}, u32[]{:S(2)}, u32[]{:S(2)}) collective-permute-start(bf16[16,256]{1,0:T(8,128)(2,1)S(1)} %collective-permute-done.7), channel_id=1, source_target_pairs={{0,15},{1,0},{2,1},{3,2},{4,3},{5,4},{6,5},{7,6},{8,7},{9,8},{10,9... | collective-permute-start | bytes 24584 | tf_op jit(solution)/shard_map/ppermute | solution.py:19
  31.0 5.8 %collective-permute-start.10 = (bf16[16,256]{1,0:T(8,128)(2,1)S(1)}, bf16[16,256]{1,0:T(8,128)(2,1)S(1)}, u32[]{:S(2)}, u32[]{:S(2)}) collective-permute-start(bf16[16,256]{1,0:T(8,128)(2,1)S(1)} %collective-permute-done.8), channel_id=1, source_target_pairs={{0,1},{1,2},{2,3},{3,4},{4,5},{5,6},{6,7},{7,8},{8,9},{9,10},{10,1... | collective-permute-start | bytes 24584 | tf_op jit(solution)/shard_map/ppermute | solution.py:16
  31.1 5.8 %collective-permute-start.11 = (bf16[16,256]{1,0:T(8,128)(2,1)S(1)}, bf16[16,256]{1,0:T(8,128)(2,1)S(1)}, u32[]{:S(2)}, u32[]{:S(2)}) collective-permute-start(bf16[16,256]{1,0:T(8,128)(2,1)S(1)} %collective-permute-done.9), channel_id=1, source_target_pairs={{0,15},{1,0},{2,1},{3,2},{4,3},{5,4},{6,5},{7,6},{8,7},{9,8},{10,9... | collective-permute-start | bytes 24584 | tf_op jit(solution)/shard_map/ppermute | solution.py:19
  36.8 5.8 %collective-permute-start.12 = (bf16[16,256]{1,0:T(8,128)(2,1)S(1)}, bf16[16,256]{1,0:T(8,128)(2,1)S(1)}, u32[]{:S(2)}, u32[]{:S(2)}) collective-permute-start(bf16[16,256]{1,0:T(8,128)(2,1)S(1)} %collective-permute-done.10), channel_id=1, source_target_pairs={{0,1},{1,2},{2,3},{3,4},{4,5},{5,6},{6,7},{7,8},{8,9},{9,10},{10,1... | collective-permute-start | bytes 24584 | tf_op jit(solution)/shard_map/ppermute | solution.py:16
  36.8 5.8 %collective-permute-start.13 = (bf16[16,256]{1,0:T(8,128)(2,1)S(1)}, bf16[16,256]{1,0:T(8,128)(2,1)S(1)}, u32[]{:S(2)}, u32[]{:S(2)}) collective-permute-start(bf16[16,256]{1,0:T(8,128)(2,1)S(1)} %collective-permute-done.11), channel_id=1, source_target_pairs={{0,15},{1,0},{2,1},{3,2},{4,3},{5,4},{6,5},{7,6},{8,7},{9,8},{10,9... | collective-permute-start | bytes 24584 | tf_op jit(solution)/shard_map/ppermute | solution.py:19
  42.6 5.8 %collective-permute-start.14 = (bf16[16,256]{1,0:T(8,128)(2,1)S(1)}, bf16[16,256]{1,0:T(8,128)(2,1)S(1)}, u32[]{:S(2)}, u32[]{:S(2)}) collective-permute-start(bf16[16,256]{1,0:T(8,128)(2,1)S(1)} %collective-permute-done.12), channel_id=1, source_target_pairs={{0,1},{1,2},{2,3},{3,4},{4,5},{5,6},{6,7},{7,8},{8,9},{9,10},{10,1... | collective-permute-start | bytes 24584 | tf_op jit(solution)/shard_map/ppermute | solution.py:16
  49.8 2.9 %collective-permute-start.15 = (bf16[64,8,256]{2,0,1:T(8,128)(2,1)S(1)}, bf16[64,8,256]{2,0,1:T(8,128)(2,1)S(1)}, u32[]{:S(2)}, u32[]{:S(2)}) collective-permute-start(bf16[64,8,256]{2,0,1:T(8,128)(2,1)S(1)} %get-tuple-element.23), channel_id=1, source_target_pairs={{0,1},{1,2},{2,3},{3,4},{4,5},{5,6},{6,7},{7,8},{8,9},{9,10},{10,1... | collective-permute-start | bytes 786440 | tf_op jit(solution)/shard_map/ppermute | solution.py:34
  51.2 3.4 %collective-permute-start.16 = (bf16[64,8,256]{2,0,1:T(8,128)(2,1)S(1)}, bf16[64,8,256]{2,0,1:T(8,128)(2,1)S(1)}, u32[]{:S(2)}, u32[]{:S(2)}) collective-permute-start(bf16[64,8,256]{2,0,1:T(8,128)(2,1)S(1)} %get-tuple-element.24), channel_id=1, source_target_pairs={{1,0},{2,1},{3,2},{4,3},{5,4},{6,5},{7,6},{8,7},{9,8},{10,9},{11,1... | collective-permute-start | bytes 786440 | tf_op jit(solution)/shard_map/ppermute | solution.py:36
  55.0 1.9 %collective-permute-start.17 = (bf16[64,32,8]{2,0,1:T(8,128)(2,1)S(1)}, bf16[64,32,8]{2,0,1:T(8,128)(2,1)S(1)}, u32[]{:S(2)}, u32[]{:S(2)}) collective-permute-start(bf16[64,32,8]{2,0,1:T(8,128)(2,1)S(1)} %get-tuple-element.19), channel_id=1, source_target_pairs={} | collective-permute-start | bytes 98312 | tf_op jit(solution)/shard_map/ppermute | solution.py:34
  55.7 1.3 collective-permute-start.18
  60.0 30.6 %copy-start.4 = (f32[2,64]{1,0:T(2,128)S(1)}, f32[2,64]{1,0:T(2,128)}, u32[]{:S(2)}) copy-start(f32[2,64]{1,0:T(2,128)} %param.14) | copy-start | bytes 1540
  60.7 33.4 %copy-start.3 = (bf16[9,64,64]{2,1,0:T(8,128)(2,1)S(1)}, bf16[9,64,64]{2,1,0:T(8,128)(2,1)}, u32[]{:S(2)}) copy-start(bf16[9,64,64]{2,1,0:T(8,128)(2,1)} %param.13) | copy-start | bytes 221188
  91.2 3.1 %collective-permute-start.19 = (bf16[64,8,256]{2,0,1:T(8,128)(2,1)S(1)}, bf16[64,8,256]{2,0,1:T(8,128)(2,1)S(1)}, u32[]{:S(2)}, u32[]{:S(2)}) collective-permute-start(bf16[64,8,256]{2,0,1:T(8,128)(2,1)S(1)} %get-tuple-element.21), channel_id=1, source_target_pairs={{0,1},{1,2},{2,3},{3,4},{4,5},{5,6},{6,7},{7,8},{8,9},{9,10},{10,1... | collective-permute-start | bytes 786440 | tf_op jit(solution)/shard_map/ppermute | solution.py:34
  92.8 3.4 %collective-permute-start.20 = (bf16[64,8,256]{2,0,1:T(8,128)(2,1)S(1)}, bf16[64,8,256]{2,0,1:T(8,128)(2,1)S(1)}, u32[]{:S(2)}, u32[]{:S(2)}) collective-permute-start(bf16[64,8,256]{2,0,1:T(8,128)(2,1)S(1)} %get-tuple-element.22), channel_id=1, source_target_pairs={{1,0},{2,1},{3,2},{4,3},{5,4},{6,5},{7,6},{8,7},{9,8},{10,9},{11,1... | collective-permute-start | bytes 786440 | tf_op jit(solution)/shard_map/ppermute | solution.py:36
  96.6 1.9 %collective-permute-start.21 = (bf16[64,32,8]{2,0,1:T(8,128)(2,1)S(1)}, bf16[64,32,8]{2,0,1:T(8,128)(2,1)S(1)}, u32[]{:S(2)}, u32[]{:S(2)}) collective-permute-start(bf16[64,32,8]{2,0,1:T(8,128)(2,1)S(1)} %get-tuple-element.15), channel_id=1, source_target_pairs={} | collective-permute-start | bytes 98312 | tf_op jit(solution)/shard_map/ppermute | solution.py:34
  97.3 1.3 collective-permute-start.22
  101.6 34.6 %copy-start.1 = (bf16[64,16,256]{2,1,0:T(8,128)(2,1)S(1)}, bf16[64,16,256]{2,1,0:T(8,128)(2,1)}, u32[]{:S(2)}) copy-start(bf16[64,16,256]{2,1,0:T(8,128)(2,1)} %param.9) | copy-start | bytes 1572868
